TPU v7x, 32 devices: a whole 2x2x4 slice. The times are simulated.
32 devices in a mesh: replica: 8 (over z, x), shard: 4 (over y, core).
Axes of the slice: x: 2, y: 2, z: 4, core: 2. Of those that a mesh axis runs over, the one named last changes fastest.
Arguments:
- tokens_in: bfloat16 [32, 256, 2048], P(('replica', 'shard')), may hold values from -6 to 6
- cotangent: bfloat16 [32, 256, 2048], P(('replica', 'shard')), may hold values from -6 to 6
- segment_ids: int32 [32, 256], P(('replica', 'shard')), may hold values from 0 to 3, never falling along the last dimension, each value on 1 to 128 neighbouring positions
- attn_gain: bfloat16 [2048], P('shard'), may hold values from 0.5 to 1.5
- w_query: bfloat16 [2048, 1024], P('shard'), may hold values from -0.125 to 0.125
- w_key: bfloat16 [2048, 256], P('shard'), may hold values from -0.125 to 0.125
- w_value: bfloat16 [2048, 256], P('shard'), may hold values from -0.125 to 0.125
- w_output: bfloat16 [1024, 2048], P('shard'), may hold values from -1.5 to 1.5
- mlp_gain: bfloat16 [2048], P('shard'), may hold values from 0.5 to 1.5
- w_gate: bfloat16 [2048, 4096], P('shard'), may hold values from -0.125 to 0.125
- w_up: bfloat16 [2048, 4096], P('shard'), may hold values from -0.125 to 0.125
- w_down: bfloat16 [4096, 2048], P('shard'), may hold values from -0.09375 to 0.09375
Outputs:
- tokens_out: bfloat16 [32, 256, 2048], P(('replica', 'shard'))
- grad_tokens: bfloat16 [32, 256, 2048], P(('replica', 'shard'))
- grad_attn_gain: float32 [2048], P('shard')
- grad_query: float32 [2048, 1024], P('shard')
- grad_key: float32 [2048, 256], P('shard')
- grad_value: float32 [2048, 256], P('shard')
- grad_output: float32 [1024, 2048], P('shard')
- grad_mlp_gain: float32 [2048], P('shard')
- grad_gate: float32 [2048, 4096], P('shard')
- grad_up: float32 [2048, 4096], P('shard')
- grad_down: float32 [4096, 2048], P('shard')
Inputs may be any that keep to these rules, and one draw needn't show every extreme that they name: `segment_ids`: in each sequence segment numbers never fall, each segment holds 1 to 128 tokens, and some segment exactly that many.
All inputs are finite; a program needn't handle non-finite values.
Results may differ from a plain program's by a relative error of at most 0.02.
Values may be sent and summed in bfloat16 or wider, within the bound.
A program may use at most 384 MiB of HBM per device.

v0:
```python
import math
import jax
import jax.numpy as jnp
from jax import lax
from jax.sharding import PartitionSpec as P

KV = 4
HD = 64
epsilon = 1e-05
theta_base = 500000.0
neg_large = -1e30


def contract(form, left_arr, right_arr):
    return jnp.einsum(form, left_arr, right_arr, preferred_element_type=jnp.float32)


def matmul(left_arr, right_arr):
    return jnp.dot(left_arr, right_arr, preferred_element_type=jnp.float32)


def positions_of(segment_ids):
    column = lax.broadcasted_iota(jnp.int32, segment_ids.shape, 1)
    starts = jnp.concatenate(
        [
            jnp.ones_like(segment_ids[:, :1]),
            (segment_ids[:, 1:] != segment_ids[:, :-1]).astype(jnp.int32),
        ],
        axis=1,
    )
    seg_start = lax.cummax(jnp.where(starts > 0, column, jnp.zeros_like(column)), axis=1)
    return column - seg_start


def rotary_tables(segment_ids, head_dim):
    positions = positions_of(segment_ids).astype(jnp.float32)
    half_dim = head_dim // 2
    exponent = jnp.arange(half_dim).astype(jnp.float32) * (2.0 / head_dim)
    inverse = theta_base ** (-exponent)
    angles = positions[:, :, None] * inverse[None, None, :]
    return (jnp.cos(angles)[:, :, None, :], jnp.sin(angles)[:, :, None, :])


def rotate(field_in, cosine, sine_tab):
    half_dim = field_in.shape[-1] // 2
    front_half = field_in[..., :half_dim]
    back_half = field_in[..., half_dim:]
    return jnp.concatenate(
        [front_half * cosine - back_half * sine_tab, front_half * sine_tab + back_half * cosine],
        axis=-1,
    )


def rotate_back(field_in, cosine, sine_tab):
    half_dim = field_in.shape[-1] // 2
    front_half = field_in[..., :half_dim]
    back_half = field_in[..., half_dim:]
    return jnp.concatenate(
        [front_half * cosine + back_half * sine_tab, back_half * cosine - front_half * sine_tab],
        axis=-1,
    )


def mask_of(segment_ids):
    length = segment_ids.shape[1]
    same_doc = segment_ids[:, :, None] == segment_ids[:, None, :]
    row_idx = lax.broadcasted_iota(jnp.int32, (length, length), 0)
    col_idx = lax.broadcasted_iota(jnp.int32, (length, length), 1)
    return (same_doc & (row_idx >= col_idx)[None])[:, None, None, :, :]


def forward_pass(tokens_in, segment_ids, weights, head_dim, kv_heads):
    attn_gain, w_query, w_key, w_value, w_output, mlp_gain, w_gate, w_up, w_down = weights
    batches, length, model_width = tokens_in.shape
    query_heads = w_query.shape[1] // head_dim
    group_size = query_heads // kv_heads
    scaling = 1.0 / math.sqrt(head_dim)
    flat_in = tokens_in.reshape(batches * length, model_width).astype(jnp.float32)
    inv_attn = lax.rsqrt(jnp.mean(flat_in * flat_in, axis=1, keepdims=True) + epsilon)
    normed_one = (flat_in * inv_attn * attn_gain.astype(jnp.float32)).astype(jnp.bfloat16)
    cosine, sine_tab = rotary_tables(segment_ids, head_dim)
    query_raw = matmul(normed_one, w_query).reshape(batches, length, query_heads, head_dim)
    key_raw = matmul(normed_one, w_key).reshape(batches, length, kv_heads, head_dim)
    query_rot = (
        rotate(query_raw, cosine, sine_tab)
        .astype(jnp.bfloat16)
        .reshape(batches, length, kv_heads, group_size, head_dim)
    )
    key_rot = rotate(key_raw, cosine, sine_tab).astype(jnp.bfloat16)
    value_rows = (
        matmul(normed_one, w_value)
        .astype(jnp.bfloat16)
        .reshape(batches, length, kv_heads, head_dim)
    )
    attn_mask = mask_of(segment_ids)
    scores = jnp.where(
        attn_mask, contract("bqkgd,bskd->bkgqs", query_rot, key_rot) * scaling, neg_large
    )
    row_max = jnp.max(scores, axis=-1, keepdims=True)
    exp_scores = jnp.exp(scores - row_max)
    row_total = jnp.sum(exp_scores, axis=-1, keepdims=True)
    log_sum = row_max + jnp.log(row_total)
    attn_probs = (exp_scores / row_total).astype(jnp.bfloat16)
    context = (
        contract("bkgqs,bskd->bqkgd", attn_probs, value_rows)
        .astype(jnp.bfloat16)
        .reshape(batches * length, query_heads * head_dim)
    )
    hidden = flat_in + matmul(context, w_output)
    inv_mlp = lax.rsqrt(jnp.mean(hidden * hidden, axis=1, keepdims=True) + epsilon)
    normed_two = (hidden * inv_mlp * mlp_gain.astype(jnp.float32)).astype(jnp.bfloat16)
    gate_pre = matmul(normed_two, w_gate)
    up_pre = matmul(normed_two, w_up)
    activated = (jax.nn.silu(gate_pre) * up_pre).astype(jnp.bfloat16)
    tokens_out = (
        (hidden + matmul(activated, w_down))
        .astype(jnp.bfloat16)
        .reshape(batches, length, model_width)
    )
    stored = (
        flat_in,
        inv_attn,
        normed_one,
        query_rot,
        key_rot,
        value_rows,
        cosine,
        sine_tab,
        attn_mask,
        log_sum,
        context,
        hidden,
        inv_mlp,
        normed_two,
        gate_pre,
        up_pre,
        activated,
    )
    return (tokens_out, stored)


def backward_pass(cotangent, stored, weights, head_dim, kv_heads):
    attn_gain, w_query, w_key, w_value, w_output, mlp_gain, w_gate, w_up, w_down = weights
    (
        flat_in,
        inv_attn,
        normed_one,
        query_rot,
        key_rot,
        value_rows,
        cosine,
        sine_tab,
        attn_mask,
        log_sum,
        context,
        hidden,
        inv_mlp,
        normed_two,
        gate_pre,
        up_pre,
        activated,
    ) = stored
    batches, length, model_width = cotangent.shape
    query_heads = w_query.shape[1] // head_dim
    group_size = query_heads // kv_heads
    scaling = 1.0 / math.sqrt(head_dim)
    grad_out = cotangent.reshape(batches * length, model_width)
    grad_down = matmul(activated.T, grad_out)
    grad_act = matmul(grad_out, w_down.T)
    sigmoid_gate = jax.nn.sigmoid(gate_pre)
    silu_gate = gate_pre * sigmoid_gate
    grad_gate_pre = (
        grad_act * up_pre * sigmoid_gate * (1.0 + gate_pre * (1.0 - sigmoid_gate))
    ).astype(jnp.bfloat16)
    grad_up_pre = (grad_act * silu_gate).astype(jnp.bfloat16)
    grad_gate = matmul(normed_two.T, grad_gate_pre)
    grad_up = matmul(normed_two.T, grad_up_pre)
    grad_two = matmul(grad_gate_pre, w_gate.T) + matmul(grad_up_pre, w_up.T)
    grad_mlp_gain = jnp.sum(grad_two * hidden * inv_mlp, axis=0)
    scaled_two = grad_two * mlp_gain.astype(jnp.float32)
    grad_hidden = grad_out.astype(jnp.float32) + inv_mlp * (
        scaled_two
        - hidden * inv_mlp * inv_mlp * jnp.mean(scaled_two * hidden, axis=1, keepdims=True)
    )
    grad_hid_bf = grad_hidden.astype(jnp.bfloat16)
    grad_output = matmul(context.T, grad_hid_bf)
    grad_context = (
        matmul(grad_hid_bf, w_output.T)
        .astype(jnp.bfloat16)
        .reshape(batches, length, kv_heads, group_size, head_dim)
    )
    scores = jnp.where(
        attn_mask, contract("bqkgd,bskd->bkgqs", query_rot, key_rot) * scaling, neg_large
    )
    probs_full = jnp.exp(scores - log_sum)
    grad_value_rows = contract("bkgqs,bqkgd->bskd", probs_full.astype(jnp.bfloat16), grad_context)
    grad_probs = contract("bqkgd,bskd->bkgqs", grad_context, value_rows)
    context_five = context.reshape(batches, length, kv_heads, group_size, head_dim).astype(
        jnp.float32
    )
    row_dot = jnp.sum(grad_context.astype(jnp.float32) * context_five, axis=-1)
    row_dot = jnp.transpose(row_dot, (0, 2, 3, 1))[..., None]
    grad_scores = (probs_full * (grad_probs - row_dot) * scaling).astype(jnp.bfloat16)
    grad_q_rot = contract("bkgqs,bskd->bqkgd", grad_scores, key_rot).reshape(
        batches, length, query_heads, head_dim
    )
    grad_k_rot = contract("bkgqs,bqkgd->bskd", grad_scores, query_rot)
    grad_q_in = (
        rotate_back(grad_q_rot, cosine, sine_tab)
        .astype(jnp.bfloat16)
        .reshape(batches * length, query_heads * head_dim)
    )
    grad_k_in = (
        rotate_back(grad_k_rot, cosine, sine_tab)
        .astype(jnp.bfloat16)
        .reshape(batches * length, kv_heads * head_dim)
    )
    grad_v_in = grad_value_rows.astype(jnp.bfloat16).reshape(batches * length, kv_heads * head_dim)
    grad_query = matmul(normed_one.T, grad_q_in)
    grad_key = matmul(normed_one.T, grad_k_in)
    grad_value = matmul(normed_one.T, grad_v_in)
    grad_one = (
        matmul(grad_q_in, w_query.T) + matmul(grad_k_in, w_key.T) + matmul(grad_v_in, w_value.T)
    )
    grad_attn_gain = jnp.sum(grad_one * flat_in * inv_attn, axis=0)
    scaled_one = grad_one * attn_gain.astype(jnp.float32)
    grad_tokens = grad_hidden + inv_attn * (
        scaled_one
        - flat_in * inv_attn * inv_attn * jnp.mean(scaled_one * flat_in, axis=1, keepdims=True)
    )
    grad_tokens = grad_tokens.astype(jnp.bfloat16).reshape(batches, length, model_width)
    return (
        grad_tokens,
        (
            grad_attn_gain,
            grad_query,
            grad_key,
            grad_value,
            grad_output,
            grad_mlp_gain,
            grad_gate,
            grad_up,
            grad_down,
        ),
    )


def per_device(
    tokens_in,
    cotangent,
    segment_ids,
    attn_gain,
    w_query,
    w_key,
    w_value,
    w_output,
    mlp_gain,
    w_gate,
    w_up,
    w_down,
):
    gathered = (
        lax.all_gather(attn_gain, "shard", axis=0, tiled=True),
        lax.all_gather(w_query, "shard", axis=0, tiled=True),
        lax.all_gather(w_key, "shard", axis=0, tiled=True),
        lax.all_gather(w_value, "shard", axis=0, tiled=True),
        lax.all_gather(w_output, "shard", axis=0, tiled=True),
        lax.all_gather(mlp_gain, "shard", axis=0, tiled=True),
        lax.all_gather(w_gate, "shard", axis=0, tiled=True),
        lax.all_gather(w_up, "shard", axis=0, tiled=True),
        lax.all_gather(w_down, "shard", axis=0, tiled=True),
    )
    tokens_out, stored = forward_pass(tokens_in, segment_ids, gathered, HD, KV)
    regathered = (
        lax.all_gather(attn_gain, "shard", axis=0, tiled=True),
        lax.all_gather(w_query, "shard", axis=0, tiled=True),
        lax.all_gather(w_key, "shard", axis=0, tiled=True),
        lax.all_gather(w_value, "shard", axis=0, tiled=True),
        lax.all_gather(w_output, "shard", axis=0, tiled=True),
        lax.all_gather(mlp_gain, "shard", axis=0, tiled=True),
        lax.all_gather(w_gate, "shard", axis=0, tiled=True),
        lax.all_gather(w_up, "shard", axis=0, tiled=True),
        lax.all_gather(w_down, "shard", axis=0, tiled=True),
    )
    grad_tokens, grads = backward_pass(cotangent, stored, regathered, HD, KV)
    shares = (
        lax.psum_scatter(
            grads[0].astype(jnp.bfloat16), "shard", scatter_dimension=0, tiled=True
        ).astype(jnp.float32),
        lax.psum_scatter(
            grads[1].astype(jnp.bfloat16), "shard", scatter_dimension=0, tiled=True
        ).astype(jnp.float32),
        lax.psum_scatter(
            grads[2].astype(jnp.bfloat16), "shard", scatter_dimension=0, tiled=True
        ).astype(jnp.float32),
        lax.psum_scatter(
            grads[3].astype(jnp.bfloat16), "shard", scatter_dimension=0, tiled=True
        ).astype(jnp.float32),
        lax.psum_scatter(
            grads[4].astype(jnp.bfloat16), "shard", scatter_dimension=0, tiled=True
        ).astype(jnp.float32),
        lax.psum_scatter(
            grads[5].astype(jnp.bfloat16), "shard", scatter_dimension=0, tiled=True
        ).astype(jnp.float32),
        lax.psum_scatter(
            grads[6].astype(jnp.bfloat16), "shard", scatter_dimension=0, tiled=True
        ).astype(jnp.float32),
        lax.psum_scatter(
            grads[7].astype(jnp.bfloat16), "shard", scatter_dimension=0, tiled=True
        ).astype(jnp.float32),
        lax.psum_scatter(
            grads[8].astype(jnp.bfloat16), "shard", scatter_dimension=0, tiled=True
        ).astype(jnp.float32),
    )
    reduced = (
        lax.psum(shares[0].astype(jnp.bfloat16), "replica").astype(jnp.float32),
        lax.psum(shares[1].astype(jnp.bfloat16), "replica").astype(jnp.float32),
        lax.psum(shares[2].astype(jnp.bfloat16), "replica").astype(jnp.float32),
        lax.psum(shares[3].astype(jnp.bfloat16), "replica").astype(jnp.float32),
        lax.psum(shares[4].astype(jnp.bfloat16), "replica").astype(jnp.float32),
        lax.psum(shares[5].astype(jnp.bfloat16), "replica").astype(jnp.float32),
        lax.psum(shares[6].astype(jnp.bfloat16), "replica").astype(jnp.float32),
        lax.psum(shares[7].astype(jnp.bfloat16), "replica").astype(jnp.float32),
        lax.psum(shares[8].astype(jnp.bfloat16), "replica").astype(jnp.float32),
    )
    return (
        tokens_out,
        grad_tokens,
        reduced[0],
        reduced[1],
        reduced[2],
        reduced[3],
        reduced[4],
        reduced[5],
        reduced[6],
        reduced[7],
        reduced[8],
    )


def solution(mesh):
    placed = (
        P(("replica", "shard"), None, None),
        P(("replica", "shard"), None, None),
        P(("replica", "shard"), None),
        P("shard"),
        P("shard", None),
        P("shard", None),
        P("shard", None),
        P("shard", None),
        P("shard"),
        P("shard", None),
        P("shard", None),
        P("shard", None),
    )
    return jax.shard_map(
        per_device,
        mesh=mesh,
        in_specs=placed,
        out_specs=(
            P(("replica", "shard"), None, None),
            P(("replica", "shard"), None, None),
            P("shard"),
            P("shard", None),
            P("shard", None),
            P("shard", None),
            P("shard", None),
            P("shard"),
            P("shard", None),
            P("shard", None),
            P("shard", None),
        ),
        check_vma=False,
    )
```

profile of v0, /device:TPU:0, one launch (start us, length us, event | category | flops | bytes accessed | tf_op | source)
XLA Modules:
  0.0 1527.5 jit_solution(17978087372400527792)
XLA Ops:
  12.9 6.2 all-gather.1
  31.2 16.2 %all-gather.10.cloned.1.call-done = bf16[2048,256]{1,0:T(8,128)(2,1)} async-done(((bf16[512,256]{1,0:T(8,128)(2,1)}), bf16[2048,256]{1,0:T(8,128)(2,1)}) %all-gather.10.cloned.1.call-update) | async-done | bytes 1048592 | tf_op jit(solution)/shard_map/all_gather | solution.py:266
  49.2 34.2 %all-gather.14.cloned.1.call-done = bf16[2048,1024]{1,0:T(8,128)(2,1)} async-done(((bf16[512,1024]{1,0:T(8,128)(2,1)}), bf16[2048,1024]{1,0:T(8,128)(2,1)}) %all-gather.14.cloned.1.call-update) | async-done | bytes 4194320 | tf_op jit(solution)/shard_map/all_gather | solution.py:264
  83.4 6.6 copy.41
  99.0 20.3 %all-gather.16.cloned.1.call-done = bf16[1024,2048]{1,0:T(8,128)(2,1)} async-done(((bf16[256,2048]{1,0:T(8,128)(2,1)}), bf16[1024,2048]{1,0:T(8,128)(2,1)}) %all-gather.16.cloned.1.call-update) | async-done | bytes 4194320 | tf_op jit(solution)/shard_map/all_gather | solution.py:267
  125.0 101.6 %all-gather.20.cloned.1.call-done = bf16[2048,4096]{1,0:T(8,128)(2,1)} async-done(((bf16[512,4096]{1,0:T(8,128)(2,1)}), bf16[2048,4096]{1,0:T(8,128)(2,1)}) %all-gather.20.cloned.1.call-update) | async-done | bytes 16777232 | tf_op jit(solution)/shard_map/all_gather | solution.py:270
  226.6 13.0 fusion.84
  239.6 94.4 %all-gather.18.cloned.1.call-done = bf16[2048,4096]{1,0:T(8,128)(2,1)} async-done(((bf16[512,4096]{1,0:T(8,128)(2,1)}), bf16[2048,4096]{1,0:T(8,128)(2,1)}) %all-gather.18.cloned.1.call-update) | async-done | bytes 16777232 | tf_op jit(solution)/shard_map/all_gather | solution.py:269
  334.0 13.4 fusion.83
  347.4 94.1 %all-gather.22.cloned.1.call-done = bf16[4096,2048]{1,0:T(8,128)(2,1)} async-done(((bf16[1024,2048]{1,0:T(8,128)(2,1)}), bf16[4096,2048]{1,0:T(8,128)(2,1)}) %all-gather.22.cloned.1.call-update) | async-done | bytes 16777232 | tf_op jit(solution)/shard_map/all_gather | solution.py:271
  441.5 13.4 multiply_convert_fusion
  454.9 12.2 fusion.85
  467.1 13.8 multiply_reduce_fusion
  518.6 12.5 convolution_convert_fusion
  531.4 12.3 convolution_convert_fusion.1
  543.8 12.4 convolution_convert_fusion.2
  556.3 39.4 %reduce-scatter.14.cloned.1.call-done = bf16[256,2048]{1,0:T(8,128)(2,1)} async-done(((bf16[1024,2048]{1,0:T(8,128)(2,1)}), bf16[256,2048]{1,0:T(8,128)(2,1)}) %reduce-scatter.14.cloned.1.call-update) | async-done | bytes 1048592 | tf_op jit(solution)/shard_map/reduce_scatter | solution.py:299
  595.7 47.7 %reduce-scatter.8.cloned.1.call-done = bf16[512,1024]{1,0:T(8,128)(2,1)} async-done(((bf16[2048,1024]{1,0:T(8,128)(2,1)}), bf16[512,1024]{1,0:T(8,128)(2,1)}) %reduce-scatter.8.cloned.1.call-update) | async-done | bytes 1048592 | tf_op jit(solution)/shard_map/reduce_scatter | solution.py:290
  643.4 127.5 %reduce-scatter.20.cloned.1.call-done = bf16[1024,2048]{1,0:T(8,128)(2,1)} async-done(((bf16[4096,2048]{1,0:T(8,128)(2,1)}), bf16[1024,2048]{1,0:T(8,128)(2,1)}) %reduce-scatter.20.cloned.1.call-update) | async-done | bytes 4194320 | tf_op jit(solution)/shard_map/reduce_scatter | solution.py:311
  770.9 127.6 %reduce-scatter.18.cloned.1.call-done = bf16[512,4096]{1,0:T(8,128)(2,1)} async-done(((bf16[2048,4096]{1,0:T(8,128)(2,1)}), bf16[512,4096]{1,0:T(8,128)(2,1)}) %reduce-scatter.18.cloned.1.call-update) | async-done | bytes 4194320 | tf_op jit(solution)/shard_map/reduce_scatter | solution.py:308
  898.6 127.5 %reduce-scatter.16.cloned.1.call-done = bf16[512,4096]{1,0:T(8,128)(2,1)} async-done(((bf16[2048,4096]{1,0:T(8,128)(2,1)}), bf16[512,4096]{1,0:T(8,128)(2,1)}) %reduce-scatter.16.cloned.1.call-update) | async-done | bytes 4194320 | tf_op jit(solution)/shard_map/reduce_scatter | solution.py:305
  1041.2 23.3 %all-reduce.2 = (bf16[512]{0:T(512)(128)(2,1)S(1)}, bf16[512]{0:T(512)(128)(2,1)S(1)}) all-reduce(bf16[512]{0:T(512)(128)(2,1)S(1)} %dynamic-slice.1, bf16[512]{0:T(512)(128)(2,1)S(1)} %dynamic-slice.3), channel_id=1, replica_groups=mesh['replica'=8,'shard'=4] {'replica'}, use_global_device_ids=true, to_apply=%region_11.12 | all-reduce | flops 1024 | bytes 4096 | tf_op jit(solution)/shard_map/psum | solution.py:316
  1069.1 9.5 fusion.14
  1078.6 421.6 %all-reduce.7.cloned.1.call-done = (bf16[512,1024]{1,0:T(8,128)(2,1)}, bf16[512,256]{1,0:T(8,128)(2,1)}, bf16[512,256]{1,0:T(8,128)(2,1)}, bf16[256,2048]{1,0:T(...) async-done(((bf16[512,1024]{1,0:T(8,128)(2,1)}, bf16[512,256]{1,0:T(8,128)(2,1)}, bf16[512,256]{1,0:T(8,128)(2,1)}, ...) | async-done | bytes 15204368 | tf_op jit(solution)/shard_map/psum | solution.py:317
  (173 shorter events, 111.5 us)
Async XLA Ops:
  7.2 21.9 %all-gather.12.cloned.1.call-start = ((), (), s32[]{:S(2)}) async-start(), calls=%async_computation.8 | async-start | bytes 1310720 | tf_op jit(solution)/shard_map/all_gather | solution.py:265
  7.9 39.4 %all-gather.10.cloned.1.call-start = ((), (), s32[]{:S(2)}) async-start(), calls=%async_computation.7 | async-start | bytes 1310720 | tf_op jit(solution)/shard_map/all_gather | solution.py:266
  8.7 74.7 %all-gather.14.cloned.1.call-start = ((), (), s32[]{:S(2)}) async-start(), calls=%async_computation.9 | async-start | bytes 5242880 | tf_op jit(solution)/shard_map/all_gather | solution.py:264
  9.4 109.9 %all-gather.16.cloned.1.call-start = ((), (), s32[]{:S(2)}) async-start(), calls=%async_computation.10 | async-start | bytes 5242880 | tf_op jit(solution)/shard_map/all_gather | solution.py:267
  10.0 216.7 %all-gather.20.cloned.1.call-start = ((), (), s32[]{:S(2)}) async-start(), calls=%async_computation.12 | async-start | bytes 20971520 | tf_op jit(solution)/shard_map/all_gather | solution.py:270
  10.6 323.4 %all-gather.18.cloned.1.call-start = ((), (), s32[]{:S(2)}) async-start(), calls=%async_computation.11 | async-start | bytes 20971520 | tf_op jit(solution)/shard_map/all_gather | solution.py:269
  11.2 13.5 copy-start
  11.2 430.3 %all-gather.22.cloned.1.call-start = ((), (), s32[]{:S(2)}) async-start(), calls=%async_computation.13 | async-start | bytes 20971520 | tf_op jit(solution)/shard_map/all_gather | solution.py:271
  11.9 544.3 %reduce-scatter.12.cloned.1.call-start = ((), (), s32[]{:S(2)}) async-start(), calls=%async_computation.16 | async-start | bytes 1310720 | tf_op jit(solution)/shard_map/reduce_scatter | solution.py:296
  25.0 65.0 %copy-start.27 = (f32[256]{0:T(256)}, f32[256]{0:T(256)S(1)}, u32[]{:S(2)}) copy-start(f32[256]{0:T(256)S(1)} %add_rsqrt_fusion.1) | copy-start | bytes 3076
  31.1 63.0 %copy-start.17 = (bf16[256,4,32]{0,2,1:T(8,128)(2,1)}, bf16[256,4,32]{0,2,1:T(8,128)(2,1)S(1)}, u32[]{:S(2)}) copy-start(bf16[256,4,32]{0,2,1:T(8,128)(2,1)S(1)} %get-tuple-element.35) | copy-start | bytes 196612
  31.2 63.0 %copy-start.19 = (bf16[256,4,32]{0,2,1:T(8,128)(2,1)}, bf16[256,4,32]{0,2,1:T(8,128)(2,1)S(1)}, u32[]{:S(2)}) copy-start(bf16[256,4,32]{0,2,1:T(8,128)(2,1)S(1)} %get-tuple-element.36) | copy-start | bytes 196612
  49.2 46.6 %copy-start.34 = (bf16[256,256]{0,1:T(8,128)(2,1)}, bf16[256,256]{0,1:T(8,128)(2,1)S(1)}, u32[]{:S(2)}) copy-start(bf16[256,256]{0,1:T(8,128)(2,1)S(1)} %convolution_convert_fusion.8) | copy-start | bytes 393220
  123.0 344.1 %copy-start.1 = (f32[256,2048]{1,0:T(8,128)}, f32[256,2048]{1,0:T(8,128)S(1)}, u32[]{:S(2)}) copy-start(f32[256,2048]{1,0:T(8,128)S(1)} %get-tuple-element.42) | copy-start | bytes 6291460
  495.3 61.0 %reduce-scatter.10.cloned.1.call-start = ((), (), s32[]{:S(2)}) async-start(), calls=%async_computation.15 | async-start | bytes 1310720 | tf_op jit(solution)/shard_map/reduce_scatter | solution.py:293
  499.1 5.3 copy-start.16
  506.8 88.8 %reduce-scatter.14.cloned.1.call-start = ((), (), s32[]{:S(2)}) async-start(), calls=%async_computation.17 | async-start | bytes 5242880 | tf_op jit(solution)/shard_map/reduce_scatter | solution.py:299
  511.2 132.2 %reduce-scatter.8.cloned.1.call-start = ((), (), s32[]{:S(2)}) async-start(), calls=%async_computation.14 | async-start | bytes 5242880 | tf_op jit(solution)/shard_map/reduce_scatter | solution.py:290
  518.6 252.3 %reduce-scatter.20.cloned.1.call-start = ((), (), s32[]{:S(2)}) async-start(), calls=%async_computation.20 | async-start | bytes 20971520 | tf_op jit(solution)/shard_map/reduce_scatter | solution.py:311
  531.2 367.4 %reduce-scatter.18.cloned.1.call-start = ((), (), s32[]{:S(2)}) async-start(), calls=%async_computation.19 | async-start | bytes 20971520 | tf_op jit(solution)/shard_map/reduce_scatter | solution.py:308
  543.7 482.3 %reduce-scatter.16.cloned.1.call-start = ((), (), s32[]{:S(2)}) async-start(), calls=%async_computation.18 | async-start | bytes 20971520 | tf_op jit(solution)/shard_map/reduce_scatter | solution.py:305
  556.2 944.0 %all-reduce.7.cloned.1.call-start = ((), (), s32[]{:S(2)}) async-start(), calls=%async_computation.21 | async-start | bytes 30408704 | tf_op jit(solution)/shard_map/psum | solution.py:317
  1507.3 4.5 copy-start.6
  1511.8 4.5 copy-start.5
  (27 other events, 59.2 us)
Sparse Core Ops, SparseCore 0:
  9.5 19.4 all-gather.11
  30.6 16.6 all-gather.9
  48.9 34.4 all-gather.13
  84.8 34.4 all-gather.15
  120.7 105.8 all-gather.19
  228.0 105.8 all-gather.17
  335.5 105.8 all-gather.21
  495.4 24.7 reduce-scatter.11
  523.3 24.7 reduce-scatter.9
  551.1 44.5 reduce-scatter.13
  598.8 44.5 reduce-scatter.7
  645.8 125.0 reduce-scatter.19
  773.5 125.0 reduce-scatter.17
  901.0 125.0 reduce-scatter.15
  1031.7 468.4 all-reduce.6
where the time goes:
time: 1530 us
  waiting for transfers between devices  1260 us (82%)
  matrix products  155 us (10%)
  blocking collectives  40.9 us (3%)
  other arithmetic  34.8 us (2%)
  local copies, waits for them, and re-layouts  20.1 us (1%)
  between operations  15.4 us (1%)
    psum x1, waiting for transfers between devices, per_device(): lax.psum(shares[1].astype(jnp.bfloat16), 'replica').astype(jnp.float32)  422 us
    dot_general x21, matrix products, matmul(): return jnp.dot(left_arr, right_arr, preferred_element_type=jnp.float32)  142 us
    reduce_scatter x1, waiting for transfers between devices, per_device(): lax.psum_scatter(grads[7].astype(jnp.bfloat16), 'shard', scatter_dimensio...  128 us
    reduce_scatter x1, waiting for transfers between devices, per_device(): lax.psum_scatter(grads[8].astype(jnp.bfloat16), 'shard', scatter_dimensio...  128 us
    reduce_scatter x1, waiting for transfers between devices, per_device(): lax.psum_scatter(grads[6].astype(jnp.bfloat16), 'shard', scatter_dimensio...  128 us
    all_gather x1, waiting for transfers between devices, per_device(): lax.all_gather(w_up, 'shard', axis=0, tiled=True)  102 us
    all_gather x1, waiting for transfers between devices, per_device(): lax.all_gather(w_gate, 'shard', axis=0, tiled=True)  94.4 us
    all_gather x1, waiting for transfers between devices, per_device(): lax.all_gather(w_down, 'shard', axis=0, tiled=True)  94.1 us
  transfers between devices with their start and end apart: 15, of which 13 were waited for; matrix products, arithmetic and copies ran while one was open for 9% of the time, Pallas kernels for 0%

commit v1 on v0

--- a/solution.py
+++ b/solution.py
@@ -314,7 +314,9 @@
     )
     reduced = (
         lax.psum(shares[0].astype(jnp.bfloat16), "replica").astype(jnp.float32),
-        lax.psum(shares[1].astype(jnp.bfloat16), "replica").astype(jnp.float32),
+        jnp.sum(lax.all_gather(shares[1].astype(jnp.bfloat16), "replica"), axis=0).astype(
+            jnp.float32
+        ),
         lax.psum(shares[2].astype(jnp.bfloat16), "replica").astype(jnp.float32),
         lax.psum(shares[3].astype(jnp.bfloat16), "replica").astype(jnp.float32),
         lax.psum(shares[4].astype(jnp.bfloat16), "replica").astype(jnp.float32),

time: 1530 us -> 1630 us (1.065)
  waiting for transfers between devices: 1260 us -> 1360 us
    all_gather x0 -> x1, waiting for transfers between devices: none -> 74.8 us  [per_device(): lax.all_gather(shares[1].astype(jnp.bfloat16), 'replica')]
    reduce_scatter x1, waiting for transfers between devices: 47.7 us -> 0.02 us  [per_device(): lax.psum_scatter(grads[1].astype(jnp.bfloat16), 'shard', scatter_dimensio...]
    reduce_scatter x1, waiting for transfers between devices: 0.02 us -> 27.7 us  [per_device(): lax.psum_scatter(grads[2].astype(jnp.bfloat16), 'shard', scatter_dimensio...]
    reduce_scatter x1, waiting for transfers between devices: 0.02 us -> 20.7 us  [per_device(): lax.psum_scatter(grads[3].astype(jnp.bfloat16), 'shard', scatter_dimensio...]
  transfers between devices with their start and end apart: 15 -> 16, of which waited for: 13 -> 15; matrix products, arithmetic and copies ran while one was open for 9% -> 8% of each run, Pallas kernels for 0% -> 0%
where the time goes in v1:
time: 1630 us
  waiting for transfers between devices  1360 us (83%)
  matrix products  154 us (9%)
  other arithmetic  41.7 us (3%)
  blocking collectives  40.6 us (2%)
  local copies, waits for them, and re-layouts  18.4 us (1%)
    psum x1, waiting for transfers between devices, per_device(): lax.psum(shares[2].astype(jnp.bfloat16), 'replica').astype(jnp.float32)  433 us
    dot_general x21, matrix products, matmul(): return jnp.dot(left_arr, right_arr, preferred_element_type=jnp.float32)  141 us
    reduce_scatter x1, waiting for transfers between devices, per_device(): lax.psum_scatter(grads[7].astype(jnp.bfloat16), 'shard', scatter_dimensio...  128 us
    reduce_scatter x1, waiting for transfers between devices, per_device(): lax.psum_scatter(grads[8].astype(jnp.bfloat16), 'shard', scatter_dimensio...  128 us
    reduce_scatter x1, waiting for transfers between devices, per_device(): lax.psum_scatter(grads[6].astype(jnp.bfloat16), 'shard', scatter_dimensio...  128 us
    all_gather x1, waiting for transfers between devices, per_device(): lax.all_gather(w_up, 'shard', axis=0, tiled=True)  102 us
    all_gather x1, waiting for transfers between devices, per_device(): lax.all_gather(w_gate, 'shard', axis=0, tiled=True)  94.4 us
    all_gather x1, waiting for transfers between devices, per_device(): lax.all_gather(w_down, 'shard', axis=0, tiled=True)  94.1 us
  transfers between devices with their start and end apart: 16, of which 15 were waited for; matrix products, arithmetic and copies ran while one was open for 8% of the time, Pallas kernels for 0%

profile of v1, /device:TPU:0, one launch (start us, length us, event | category | flops | bytes accessed | tf_op | source)
XLA Modules:
  0.0 1627.4 jit_solution(2525651051474912317)
XLA Ops:
  31.2 16.2 all-gather.12.cloned.1.call-done
  49.2 34.2 %all-gather.16.cloned.1.call-done = bf16[2048,1024]{1,0:T(8,128)(2,1)} async-done(((bf16[512,1024]{1,0:T(8,128)(2,1)}), bf16[2048,1024]{1,0:T(8,128)(2,1)}) %all-gather.16.cloned.1.call-update) | async-done | bytes 4194320 | tf_op jit(solution)/shard_map/all_gather | solution.py:264
  99.0 20.3 %all-gather.18.cloned.1.call-done = bf16[1024,2048]{1,0:T(8,128)(2,1)} async-done(((bf16[256,2048]{1,0:T(8,128)(2,1)}), bf16[1024,2048]{1,0:T(8,128)(2,1)}) %all-gather.18.cloned.1.call-update) | async-done | bytes 4194320 | tf_op jit(solution)/shard_map/all_gather | solution.py:267
  125.0 101.6 %all-gather.22.cloned.1.call-done = bf16[2048,4096]{1,0:T(8,128)(2,1)} async-done(((bf16[512,4096]{1,0:T(8,128)(2,1)}), bf16[2048,4096]{1,0:T(8,128)(2,1)}) %all-gather.22.cloned.1.call-update) | async-done | bytes 16777232 | tf_op jit(solution)/shard_map/all_gather | solution.py:270
  226.6 13.0 fusion.84
  239.6 94.4 %all-gather.20.cloned.1.call-done = bf16[2048,4096]{1,0:T(8,128)(2,1)} async-done(((bf16[512,4096]{1,0:T(8,128)(2,1)}), bf16[2048,4096]{1,0:T(8,128)(2,1)}) %all-gather.20.cloned.1.call-update) | async-done | bytes 16777232 | tf_op jit(solution)/shard_map/all_gather | solution.py:269
  334.0 13.4 fusion.83
  347.4 94.1 %all-gather.24.cloned.1.call-done = bf16[4096,2048]{1,0:T(8,128)(2,1)} async-done(((bf16[1024,2048]{1,0:T(8,128)(2,1)}), bf16[4096,2048]{1,0:T(8,128)(2,1)}) %all-gather.24.cloned.1.call-update) | async-done | bytes 16777232 | tf_op jit(solution)/shard_map/all_gather | solution.py:271
  441.5 13.3 multiply_convert_fusion
  454.8 12.2 fusion.85
  467.0 13.8 multiply_reduce_fusion
  517.1 12.2 convolution_convert_fusion
  529.5 12.3 convolution_convert_fusion.1
  541.9 12.2 convolution_convert_fusion.2
  554.8 20.7 %reduce-scatter.12.cloned.1.call-done = bf16[512,256]{1,0:T(8,128)(2,1)} async-done(((bf16[2048,256]{1,0:T(8,128)(2,1)}), bf16[512,256]{1,0:T(8,128)(2,1)}) %reduce-scatter.12.cloned.1.call-update) | async-done | bytes 262160 | tf_op jit(solution)/shard_map/reduce_scatter | solution.py:296
  575.4 27.7 %reduce-scatter.10.cloned.1.call-done = bf16[512,256]{1,0:T(8,128)(2,1)} async-done(((bf16[2048,256]{1,0:T(8,128)(2,1)}), bf16[512,256]{1,0:T(8,128)(2,1)}) %reduce-scatter.10.cloned.1.call-update) | async-done | bytes 262160 | tf_op jit(solution)/shard_map/reduce_scatter | solution.py:293
  603.2 47.7 %reduce-scatter.14.cloned.1.call-done = bf16[256,2048]{1,0:T(8,128)(2,1)} async-done(((bf16[1024,2048]{1,0:T(8,128)(2,1)}), bf16[256,2048]{1,0:T(8,128)(2,1)}) %reduce-scatter.14.cloned.1.call-update) | async-done | bytes 1048592 | tf_op jit(solution)/shard_map/reduce_scatter | solution.py:299
  650.8 127.5 %reduce-scatter.20.cloned.1.call-done = bf16[1024,2048]{1,0:T(8,128)(2,1)} async-done(((bf16[4096,2048]{1,0:T(8,128)(2,1)}), bf16[1024,2048]{1,0:T(8,128)(2,1)}) %reduce-scatter.20.cloned.1.call-update) | async-done | bytes 4194320 | tf_op jit(solution)/shard_map/reduce_scatter | solution.py:311
  778.4 127.7 %reduce-scatter.18.cloned.1.call-done = bf16[512,4096]{1,0:T(8,128)(2,1)} async-done(((bf16[2048,4096]{1,0:T(8,128)(2,1)}), bf16[512,4096]{1,0:T(8,128)(2,1)}) %reduce-scatter.18.cloned.1.call-update) | async-done | bytes 4194320 | tf_op jit(solution)/shard_map/reduce_scatter | solution.py:308
  906.0 127.5 %reduce-scatter.16.cloned.1.call-done = bf16[512,4096]{1,0:T(8,128)(2,1)} async-done(((bf16[2048,4096]{1,0:T(8,128)(2,1)}), bf16[512,4096]{1,0:T(8,128)(2,1)}) %reduce-scatter.16.cloned.1.call-update) | async-done | bytes 4194320 | tf_op jit(solution)/shard_map/reduce_scatter | solution.py:305
  1048.7 23.0 %all-reduce.2 = (bf16[512]{0:T(512)(128)(2,1)S(1)}, bf16[512]{0:T(512)(128)(2,1)S(1)}) all-reduce(bf16[512]{0:T(512)(128)(2,1)S(1)} %dynamic-slice.1, bf16[512]{0:T(512)(128)(2,1)S(1)} %dynamic-slice.3), channel_id=1, replica_groups=mesh['replica'=8,'shard'=4] {'replica'}, use_global_device_ids=true, to_apply=%region_11.12 | all-reduce | flops 1024 | bytes 4096 | tf_op jit(solution)/shard_map/psum | solution.py:316
  1076.2 9.3 fusion.14
  1085.6 74.8 %all-gather.26.cloned.1.call-done = bf16[4096,1024]{1,0:T(8,128)(2,1)} async-done(((bf16[512,1024]{1,0:T(8,128)(2,1)}), bf16[4096,1024]{1,0:T(8,128)(2,1)}) %all-gather.26.cloned.1.call-update) | async-done | bytes 8388624 | tf_op jit(solution)/shard_map/all_gather | solution.py:317
  1167.6 433.1 %all-reduce.7.cloned.1.call-done = (bf16[512,256]{1,0:T(8,128)(2,1)}, bf16[512,256]{1,0:T(8,128)(2,1)}, bf16[256,2048]{1,0:T(8,128)(2,1)}, bf16[512,4096]{1,0:T(...) async-done(((bf16[512,256]{1,0:T(8,128)(2,1)}, bf16[512,256]{1,0:T(8,128)(2,1)}, bf16[256,2048]{1,0:T(8,128)(2,1)}, bf16[512,4096]{1,0:T(8,128)(2,1)}, ...) | async-done | bytes 14155792 | tf_op jit(solution)/shard_map/psum | solution.py:320
  (171 shorter events, 129.9 us)
Async XLA Ops:
  7.2 21.9 %all-gather.14.cloned.1.call-start = ((), (), s32[]{:S(2)}) async-start(), calls=%async_computation.8 | async-start | bytes 1310720 | tf_op jit(solution)/shard_map/all_gather | solution.py:265
  7.9 39.4 %all-gather.12.cloned.1.call-start = ((), (), s32[]{:S(2)}) async-start(), calls=%async_computation.7 | async-start | bytes 1310720 | tf_op jit(solution)/shard_map/all_gather | solution.py:266
  8.7 74.7 %all-gather.16.cloned.1.call-start = ((), (), s32[]{:S(2)}) async-start(), calls=%async_computation.9 | async-start | bytes 5242880 | tf_op jit(solution)/shard_map/all_gather | solution.py:264
  9.4 109.9 %all-gather.18.cloned.1.call-start = ((), (), s32[]{:S(2)}) async-start(), calls=%async_computation.10 | async-start | bytes 5242880 | tf_op jit(solution)/shard_map/all_gather | solution.py:267
  10.0 216.7 %all-gather.22.cloned.1.call-start = ((), (), s32[]{:S(2)}) async-start(), calls=%async_computation.12 | async-start | bytes 20971520 | tf_op jit(solution)/shard_map/all_gather | solution.py:270
  10.6 323.4 %all-gather.20.cloned.1.call-start = ((), (), s32[]{:S(2)}) async-start(), calls=%async_computation.11 | async-start | bytes 20971520 | tf_op jit(solution)/shard_map/all_gather | solution.py:269
  11.2 13.5 copy-start
  11.2 430.3 %all-gather.24.cloned.1.call-start = ((), (), s32[]{:S(2)}) async-start(), calls=%async_computation.13 | async-start | bytes 20971520 | tf_op jit(solution)/shard_map/all_gather | solution.py:271
  11.9 542.3 %reduce-scatter.8.cloned.1.call-start = ((), (), s32[]{:S(2)}) async-start(), calls=%async_computation.14 | async-start | bytes 5242880 | tf_op jit(solution)/shard_map/reduce_scatter | solution.py:290
  25.0 65.0 %copy-start.24 = (f32[256]{0:T(256)}, f32[256]{0:T(256)S(1)}, u32[]{:S(2)}) copy-start(f32[256]{0:T(256)S(1)} %add_rsqrt_fusion.1) | copy-start | bytes 3076
  31.1 63.0 %copy-start.14 = (bf16[256,4,32]{0,2,1:T(8,128)(2,1)}, bf16[256,4,32]{0,2,1:T(8,128)(2,1)S(1)}, u32[]{:S(2)}) copy-start(bf16[256,4,32]{0,2,1:T(8,128)(2,1)S(1)} %get-tuple-element.34) | copy-start | bytes 196612
  31.2 63.0 %copy-start.16 = (bf16[256,4,32]{0,2,1:T(8,128)(2,1)}, bf16[256,4,32]{0,2,1:T(8,128)(2,1)S(1)}, u32[]{:S(2)}) copy-start(bf16[256,4,32]{0,2,1:T(8,128)(2,1)S(1)} %get-tuple-element.35) | copy-start | bytes 196612
  49.2 46.7 %copy-start.31 = (bf16[256,256]{0,1:T(8,128)(2,1)}, bf16[256,256]{0,1:T(8,128)(2,1)S(1)}, u32[]{:S(2)}) copy-start(bf16[256,256]{0,1:T(8,128)(2,1)S(1)} %convolution_convert_fusion.8) | copy-start | bytes 393220
  123.0 344.0 %copy-start.1 = (f32[256,2048]{1,0:T(8,128)}, f32[256,2048]{1,0:T(8,128)S(1)}, u32[]{:S(2)}) copy-start(f32[256,2048]{1,0:T(8,128)S(1)} %get-tuple-element.41) | copy-start | bytes 6291460
  502.8 72.7 %reduce-scatter.12.cloned.1.call-start = ((), (), s32[]{:S(2)}) async-start(), calls=%async_computation.16 | async-start | bytes 1310720 | tf_op jit(solution)/shard_map/reduce_scatter | solution.py:296
  508.4 94.8 %reduce-scatter.10.cloned.1.call-start = ((), (), s32[]{:S(2)}) async-start(), calls=%async_computation.15 | async-start | bytes 1310720 | tf_op jit(solution)/shard_map/reduce_scatter | solution.py:293
  512.6 138.2 %reduce-scatter.14.cloned.1.call-start = ((), (), s32[]{:S(2)}) async-start(), calls=%async_computation.17 | async-start | bytes 5242880 | tf_op jit(solution)/shard_map/reduce_scatter | solution.py:299
  517.0 261.4 %reduce-scatter.20.cloned.1.call-start = ((), (), s32[]{:S(2)}) async-start(), calls=%async_computation.20 | async-start | bytes 20971520 | tf_op jit(solution)/shard_map/reduce_scatter | solution.py:311
  529.3 376.8 %reduce-scatter.18.cloned.1.call-start = ((), (), s32[]{:S(2)}) async-start(), calls=%async_computation.19 | async-start | bytes 20971520 | tf_op jit(solution)/shard_map/reduce_scatter | solution.py:308
  541.8 491.7 %reduce-scatter.16.cloned.1.call-start = ((), (), s32[]{:S(2)}) async-start(), calls=%async_computation.18 | async-start | bytes 20971520 | tf_op jit(solution)/shard_map/reduce_scatter | solution.py:305
  554.1 606.3 %all-gather.26.cloned.1.call-start = ((), (), s32[]{:S(2)}) async-start(), calls=%async_computation.21 | async-start | bytes 9437184 | tf_op jit(solution)/shard_map/all_gather | solution.py:317
  554.7 1046.0 %all-reduce.7.cloned.1.call-start = ((), (), s32[]{:S(2)}) async-start(), calls=%async_computation.22 | async-start | bytes 28311552 | tf_op jit(solution)/shard_map/psum | solution.py:320
  1600.7 6.5 copy-start.7
  1607.2 4.5 copy-start.6
  (25 other events, 57.0 us)
Sparse Core Ops, SparseCore 0:
  9.5 19.4 all-gather.13
  30.6 16.6 all-gather.11
  48.9 34.4 all-gather.15
  84.8 34.4 all-gather.17
  120.7 105.8 all-gather.21
  228.0 105.8 all-gather.19
  335.5 105.8 all-gather.23
  502.9 44.5 reduce-scatter.7
  550.6 24.7 reduce-scatter.11
  578.4 24.7 reduce-scatter.9
  606.3 44.5 reduce-scatter.13
  653.3 125.0 reduce-scatter.19
  781.0 125.0 reduce-scatter.17
  908.5 125.0 reduce-scatter.15
  1035.5 124.8 all-gather.25
  1165.7 434.9 all-reduce.6
